TPU v7x, 1024 devices: a whole 4x4x32 slice. The times are simulated.
1024 devices in a mesh: gx: 16 (over z_hi, y), gy: 8 (over x, core), gz: 8 (over z_lo).
Axes of the slice: x: 4, y: 4, z: 32 (z_hi: 4, z_lo: 8; z = z_hi * 8 + z_lo), core: 2. Of those that a mesh axis runs over, the one named last changes fastest.
Arguments:
- conserved: float32 [5, 256, 128, 1024], P(None, 'gx', 'gy', 'gz'), as said below
Outputs:
- advanced: float32 [5, 256, 128, 1024], P(None, 'gx', 'gy', 'gz')
Inputs may be any that keep to these rules, and one draw needn't show every extreme that they name: `conserved`: every cell has positive density and positive pressure (energy above the kinetic energy).
All inputs are finite; a program needn't handle non-finite values. Where the computation divides by a largest or mean magnitude, that divisor is 1e-20 or more.
Results may differ from a plain program's by a relative error of at most 0.000066.
Values sent between devices are 32-bit elements; how exact they have to be, the bound alone decides.
A program may use at most 32 MiB of HBM per device.

v0:
```python
import jax
import jax.numpy as jnp
from jax import lax
from jax.sharding import Mesh
from jax.sharding import PartitionSpec as P

GX = ("gx_0", "gx_1")
GY = ("gy_0", "gy_1")
GX_GY_GZ = ("gx_0", "gx_1", "gy_0", "gy_1", "gz")


gamma_gas = 1.4
weno_eps = 1e-06
courant = 0.4


def by_axis(shard, axes):
    for axis in axes:
        shard = lax.pmax(shard, axis)
    return shard


def padded(shard, sides, width):
    for axis, dim in sides:
        devices, length = (lax.axis_size(axis), shard.shape[dim])
        up = [(i, (i + 1) % devices) for i in range(devices)]
        down = [(j, i) for i, j in up]
        last = lax.slice_in_dim(shard, length - width, length, axis=dim)
        first = lax.slice_in_dim(shard, 0, width, axis=dim)
        before = lax.ppermute(last, axis, up)
        after = lax.ppermute(first, axis, down)
        shard = jnp.concatenate([before, shard, after], axis=dim)
    return shard


def primitives(components):
    density = components[0]
    vel_normal = components[1] / density
    vel_first = components[2] / density
    vel_second = components[3] / density
    kinetic = 0.5 * (vel_normal * vel_normal + vel_first * vel_first + vel_second * vel_second)
    pressure = (gamma_gas - 1.0) * (components[4] - density * kinetic)
    return (density, vel_normal, vel_first, vel_second, kinetic, pressure)


def multiply_rows(matrix, vector):
    result = []
    for matrix_row in matrix:
        accum = None
        for coefficient, component in zip(matrix_row, vector):
            if coefficient is None:
                continue
            product_term = component * coefficient
            accum = product_term if accum is None else accum + product_term
        result.append(accum)
    return result


def weno_face(far_left, near_left, centre, near_right, far_right):
    poly_left = (2.0 * far_left - 7.0 * near_left + 11.0 * centre) / 6.0
    poly_mid = (-near_left + 5.0 * centre + 2.0 * near_right) / 6.0
    poly_right = (2.0 * centre + 5.0 * near_right - far_right) / 6.0
    diff_one = far_left - 2.0 * near_left + centre
    diff_two = far_left - 4.0 * near_left + 3.0 * centre
    smooth_left = 13.0 / 12.0 * diff_one * diff_one + 0.25 * diff_two * diff_two
    diff_one = near_left - 2.0 * centre + near_right
    diff_two = near_left - near_right
    smooth_mid = 13.0 / 12.0 * diff_one * diff_one + 0.25 * diff_two * diff_two
    diff_one = centre - 2.0 * near_right + far_right
    diff_two = 3.0 * centre - 4.0 * near_right + far_right
    smooth_right = 13.0 / 12.0 * diff_one * diff_one + 0.25 * diff_two * diff_two
    weight_left = 0.1 / ((weno_eps + smooth_left) * (weno_eps + smooth_left))
    weight_mid = 0.6 / ((weno_eps + smooth_mid) * (weno_eps + smooth_mid))
    weight_right = 0.3 / ((weno_eps + smooth_right) * (weno_eps + smooth_right))
    return (weight_left * poly_left + weight_mid * poly_mid + weight_right * poly_right) / (
        weight_left + weight_mid + weight_right
    )


def face_divergence(components, line_axis, wave_speed, cell_count):
    length = components[0].shape[line_axis] - 6
    face_count = length + 1

    def window(array_item, start, count):
        return lax.slice_in_dim(array_item, start, start + count, axis=line_axis)

    density, vel_normal, vel_first, vel_second, kinetic, pressure = primitives(components)
    fluxes = [
        components[1],
        components[1] * vel_normal + pressure,
        components[2] * vel_normal,
        components[3] * vel_normal,
        (components[4] + pressure) * vel_normal,
    ]
    split_plus = [
        0.5 * (flux + wave_speed * component) for flux, component in zip(fluxes, components)
    ]
    split_minus = [
        0.5 * (flux - wave_speed * component) for flux, component in zip(fluxes, components)
    ]
    face_mean = [
        0.5 * (window(component, 2, face_count) + window(component, 3, face_count))
        for component in components
    ]
    mean_density, mean_normal, mean_first, mean_second, mean_kinetic, mean_pressure = primitives(
        face_mean
    )
    enthalpy = (face_mean[4] + mean_pressure) / mean_density
    sound_speed = jnp.sqrt(gamma_gas * mean_pressure / mean_density)
    inv_sound = 1.0 / sound_speed
    coef_one = (gamma_gas - 1.0) / (sound_speed * sound_speed)
    coef_two = coef_one * mean_kinetic
    left_rows = [
        [
            0.5 * (coef_two + mean_normal * inv_sound),
            -0.5 * (coef_one * mean_normal + inv_sound),
            -0.5 * coef_one * mean_first,
            -0.5 * coef_one * mean_second,
            0.5 * coef_one,
        ],
        [-mean_first, None, 1.0, None, None],
        [-mean_second, None, None, 1.0, None],
        [
            1.0 - coef_two,
            coef_one * mean_normal,
            coef_one * mean_first,
            coef_one * mean_second,
            -coef_one,
        ],
        [
            0.5 * (coef_two - mean_normal * inv_sound),
            -0.5 * (coef_one * mean_normal - inv_sound),
            -0.5 * coef_one * mean_first,
            -0.5 * coef_one * mean_second,
            0.5 * coef_one,
        ],
    ]
    right_cols = [
        [1.0, None, None, 1.0, 1.0],
        [mean_normal - sound_speed, None, None, mean_normal, mean_normal + sound_speed],
        [mean_first, 1.0, None, mean_first, mean_first],
        [mean_second, None, 1.0, mean_second, mean_second],
        [
            enthalpy - mean_normal * sound_speed,
            mean_first,
            mean_second,
            mean_kinetic,
            enthalpy + mean_normal * sound_speed,
        ],
    ]
    positive = [
        multiply_rows(
            left_rows, [window(component, offset, face_count) for component in split_plus]
        )
        for offset in range(5)
    ]
    negative = [
        multiply_rows(
            left_rows, [window(component, offset, face_count) for component in split_minus]
        )
        for offset in range(1, 6)
    ]
    wave_sums = []
    for wave_index in range(5):
        upwind = weno_face(*[positive[offset][wave_index] for offset in range(5)])
        downwind = weno_face(*[negative[offset][wave_index] for offset in (4, 3, 2, 1, 0)])
        wave_sums.append(upwind + downwind)
    face_flux = multiply_rows(right_cols, wave_sums)
    return [-(window(flux, 1, length) - window(flux, 0, length)) * cell_count for flux in face_flux]


def component_order(direction):
    if direction == 0:
        return [0, 1, 2, 3, 4]
    if direction == 1:
        return [0, 2, 1, 3, 4]
    return [0, 3, 1, 2, 4]


def direction_terms(padded_slab, line_axis, direction, wave_speed, cell_count):
    comp_order = component_order(direction)
    result = face_divergence(
        [padded_slab[index] for index in comp_order], line_axis, wave_speed, cell_count
    )
    placed = [None] * 5
    for index, target in enumerate(comp_order):
        placed[target] = result[index]
    return jnp.stack(placed)


def per_device(conserved):
    cells_x = conserved.shape[1] * lax.axis_size(GX)
    cells_y = conserved.shape[2] * lax.axis_size(GY)
    cells_z = conserved.shape[3] * lax.axis_size("gz")
    components = [conserved[index] for index in range(5)]
    density, vel_one, vel_two, vel_three, kinetic, pressure = primitives(components)
    sound_speed = jnp.sqrt(gamma_gas * pressure / density)
    local_x = jnp.max(jnp.abs(vel_one) + sound_speed)
    local_y = jnp.max(jnp.abs(vel_two) + sound_speed)
    local_z = jnp.max(jnp.abs(vel_three) + sound_speed)
    speed_x, speed_y, speed_z = (
        by_axis(local_x, GX_GY_GZ),
        by_axis(local_y, GX_GY_GZ),
        by_axis(local_z, GX_GY_GZ),
    )
    step = courant / (speed_x * cells_x + speed_y * cells_y + speed_z * cells_z)
    along_x = padded(conserved, ((GX, 1),), 3)
    tendency = direction_terms(along_x, 0, 0, speed_x, cells_x)
    along_y = padded(conserved, ((GY, 2),), 3)
    tendency = tendency + direction_terms(along_y, 1, 1, speed_y, cells_y)
    along_z = padded(conserved, (("gz", 3),), 3)
    tendency = tendency + direction_terms(along_z, 2, 2, speed_z, cells_z)
    return conserved + step * tendency


def solution(mesh):
    finer = Mesh(
        mesh.devices.reshape(4, 4, 4, 2, mesh.shape["gz"]), ("gx_0", "gx_1", "gy_0", "gy_1", "gz")
    )
    placed = (P(None, GX, GY, "gz"),)
    return jax.shard_map(
        per_device, mesh=finer, in_specs=placed, out_specs=P(None, GX, GY, "gz"), check_vma=False
    )
```

profile of v0, /device:TPU:1, one launch (start us, length us, event | category | flops | bytes accessed | tf_op | source)
XLA Modules:
  0.0 176.4 jit_solution(11887352634842444794)
XLA Ops:
  0.0 1.5 fusion.481
  1.5 0.6 copy.22
  2.1 13.7 %collective-permute-start.5 = (f32[5,16,16,3]{2,1,3,0:T(8,128)S(1)}, f32[5,16,16,3]{2,1,3,0:T(8,128)S(1)}, u32[]{:S(2)}, u32[]{:S(2)}) collective-permute-start(f32[5,16,16,3]{2,1,3,0:T(8,128)S(1)} %copy.22), channel_id=1, source_target_pairs={{1,0},{2,1},{3,2},{4,3},{5,4},{6,5},{7,6},{0,7},{9,8},{10,9},{11,1... | collective-permute-start | bytes 46088 | tf_op jit(solution)/shard_map/ppermute | solution.py:31
  15.8 0.6 copy.21
  16.4 1.9 %collective-permute-start.4 = (f32[5,16,16,3]{2,1,3,0:T(8,128)S(1)}, f32[5,16,16,3]{2,1,3,0:T(8,128)}, u32[]{:S(2)}, u32[]{:S(2)}) collective-permute-start(f32[5,16,16,3]{2,1,3,0:T(8,128)S(1)} %copy.21), channel_id=1, source_target_pairs={{0,1},{1,2},{2,3},{3,4},{4,5},{5,6},{6,7},{7,0},{8,9},{9,10},{10,1... | collective-permute-start | bytes 46088 | tf_op jit(solution)/shard_map/ppermute | solution.py:30
  18.3 0.2 copy.19
  18.5 0.7 fusion.479
  19.2 2.1 %collective-permute-start.2 = (f32[5,16,3,128]{3,1,2,0:T(8,128)}, f32[5,16,3,128]{3,1,2,0:T(8,128)S(1)}, u32[]{:S(2)}, u32[]{:S(2)}) collective-permute-start(f32[5,16,3,128]{3,1,2,0:T(8,128)} %get-tuple-element.108), channel_id=1, source_target_pairs={{0,8},{8,16},{16,24},{24,32},{32,40},{40,48},{48,56},{56,0},{1,9},... | collective-permute-start | bytes 368648 | tf_op jit(solution)/shard_map/ppermute | solution.py:30
  21.3 2.3 %collective-permute-start.3 = (f32[5,16,3,128]{3,1,2,0:T(8,128)}, f32[5,16,3,128]{3,1,2,0:T(8,128)S(1)}, u32[]{:S(2)}, u32[]{:S(2)}) collective-permute-start(f32[5,16,3,128]{3,1,2,0:T(8,128)} %get-tuple-element.107), channel_id=1, source_target_pairs={{8,0},{16,8},{24,16},{32,24},{40,32},{48,40},{56,48},{0,56},{9,1},... | collective-permute-start | bytes 368648 | tf_op jit(solution)/shard_map/ppermute | solution.py:31
  23.6 0.1 fusion.480
  23.6 15.4 %collective-permute-start.1 = (f32[5,3,16,128]{3,1,2,0:T(4,128)S(1)}, f32[5,3,16,128]{3,1,2,0:T(4,128)S(1)}, u32[]{:S(2)}, u32[]{:S(2)}) collective-permute-start(f32[5,3,16,128]{3,1,2,0:T(4,128)S(1)} %get-tuple-element.112), channel_id=1, source_target_pairs={{64,0},{128,64},{192,128},{256,192},{320,256},{384,320},{448,384},... | collective-permute-start | bytes 368648 | tf_op jit(solution)/shard_map/ppermute | solution.py:31
  39.0 0.8 add_reduce_fusion.1
  39.8 20.5 %all-reduce.3 = (f32[]{:T(128)}, f32[]{:T(128)}, f32[]{:T(128)}) all-reduce(f32[]{:T(128)} %get-tuple-element.6, f32[]{:T(128)} %get-tuple-element.7, f32[]{:T(128)} %get-tuple-element.5), channel_id=1, replica_groups=mesh['gx_0'=4,'gx_1'=4,'gy_0'=4,'gy_1'=2,'gz'=8] {'gx_0'}, use_global_device_ids=true, to_apply=%region_13.0 | all-reduce | flops 3 | bytes 24 | tf_op jit(solution)/shard_map/pmax | solution.py:19
  60.3 6.7 %all-reduce.2 = (f32[]{:T(128)}, f32[]{:T(128)}, f32[]{:T(128)}) all-reduce(f32[]{:T(128)} %get-tuple-element.17, f32[]{:T(128)} %get-tuple-element.18, f32[]{:T(128)} %get-tuple-element.19), channel_id=1, replica_groups=mesh['gx_0'=4,'gx_1'=4,'gy_0'=4,'gy_1'=2,'gz'=8] {'gx_1'}, use_global_device_ids=true, to_apply=%region_14.0 | all-reduce | flops 3 | bytes 24 | tf_op jit(solution)/shard_map/pmax | solution.py:19
  67.0 26.9 %all-reduce.1 = (f32[]{:T(128)}, f32[]{:T(128)}, f32[]{:T(128)}) all-reduce(f32[]{:T(128)} %get-tuple-element.14, f32[]{:T(128)} %get-tuple-element.15, f32[]{:T(128)} %get-tuple-element.16), channel_id=1, replica_groups=mesh['gx_0'=4,'gx_1'=4,'gy_0'=4,'gy_1'=2,'gz'=8] {'gy_0'}, use_global_device_ids=true, to_apply=%region_15.0 | all-reduce | flops 3 | bytes 24 | tf_op jit(solution)/shard_map/pmax | solution.py:19
  93.9 8.2 %all-reduce.4 = (f32[]{:T(128)}, f32[]{:T(128)}, f32[]{:T(128)}) all-reduce(f32[]{:T(128)} %get-tuple-element.11, f32[]{:T(128)} %get-tuple-element.12, f32[]{:T(128)} %get-tuple-element.13), channel_id=1, replica_groups=mesh['gx_0'=4,'gx_1'=4,'gy_0'=4,'gy_1'=2,'gz'=8] {'gy_1'}, use_global_device_ids=true, to_apply=%region_16.0 | all-reduce | flops 3 | bytes 24 | tf_op jit(solution)/shard_map/pmax | solution.py:19
  102.1 23.7 %all-reduce = (f32[]{:T(128)}, f32[]{:T(128)}, f32[]{:T(128)}) all-reduce(f32[]{:T(128)} %get-tuple-element.20, f32[]{:T(128)} %get-tuple-element.21, f32[]{:T(128)} %get-tuple-element.22), channel_id=1, replica_groups=mesh['gx_0'=4,'gx_1'=4,'gy_0'=4,'gy_1'=2,'gz'=8] {'gz'}, use_global_device_ids=true, to_apply=%region_17.0 | all-reduce | flops 3 | bytes 24 | tf_op jit(solution)/shard_map/pmax | solution.py:19
  127.8 3.6 %collective-permute-start = (f32[5,3,16,128]{3,1,2,0:T(4,128)S(1)}, f32[5,3,16,128]{3,1,2,0:T(4,128)S(1)}, u32[]{:S(2)}, u32[]{:S(2)}) collective-permute-start(f32[5,3,16,128]{3,1,2,0:T(4,128)S(1)} %get-tuple-element.111), channel_id=1, source_target_pairs={{0,64},{64,128},{128,192},{192,256},{256,320},{320,384},{384,448},... | collective-permute-start | bytes 368648 | tf_op jit(solution)/shard_map/ppermute | solution.py:30
  131.5 0.6 copy.18
  132.1 1.4 copy.16
  133.5 0.6 pad_maximum_fusion
  134.1 0.1 slice_bitcast_fusion.4
  134.2 0.8 subtract_multiply_fusion
  135.0 1.0 add_multiply_fusion.4
  136.0 17.0 %multiply_add_fusion.1 = (f32[16,16,129]{2,0,1:T(8,128)S(1)}, f32[16,16,129]{2,0,1:T(8,128)S(1)}, f32[16,16,129]{2,0,1:T(8,128)S(1)}, f32[16,16,129]{2,0,1:T(8,1...) fusion(f32[16,16,134]{2,0,1:T(8,128)S(1)} %get-tuple-element.76, ...), kind=kLoop, calls=%fused_computation.269 | loop fusion | flops 32594688 | bytes 9246720 | tf_op jit(solution)/shard_map/add | solution.py:54
  153.1 0.3 multiply_add_fusion.2
  153.3 0.1 fusion.419
  153.4 0.1 fusion.415
  153.6 0.1 fusion.411
  153.7 0.1 fusion.407
  153.8 0.2 constant_dynamic-update-slice_fusion.3
  154.0 0.1 slice_bitcast_fusion.13
  154.1 0.8 subtract_multiply_fusion.12
  154.9 0.9 add_multiply_fusion.18
  155.8 0.2 divide_sqrt_fusion.2
  156.0 6.5 %multiply_add_fusion.12 = (f32[16,17,128]{2,0,1:T(8,128)S(1)}, f32[16,17,128]{2,0,1:T(8,128)S(1)}, f32[16,17,128]{2,0,1:T(8,128)S(1)}, f32[16,17,128]{2,0,1:T(8,...) fusion(f32[16,17,128]{2,0,1:T(8,128)S(1)} %get-tuple-element.34, ...), kind=kLoop, calls=%fused_computation.749 | loop fusion | flops 33910784 | bytes 8773632 | tf_op jit(solution)/shard_map/add | solution.py:54
  162.5 0.1 multiply_add_fusion.13
  162.7 0.2 pad_maximum_fusion.1
  162.8 0.8 subtract_multiply_fusion.6
  163.6 0.9 add_multiply_fusion.11
  164.5 0.1 constant_dynamic-update-slice_fusion
  164.6 0.1 fusion.268
  164.7 0.1 fusion.265
  164.8 9.6 %multiply_add_fusion.6 = (f32[17,16,128]{2,0,1:T(8,128)S(1)}, f32[17,16,128]{2,0,1:T(8,128)S(1)}, f32[17,16,128]{2,0,1:T(8,128)S(1)}, f32[17,16,128]{2,0,1:T(8,1...) fusion(f32[17,16,128]{2,0,1:T(8,128)S(1)} %get-tuple-element.46, ...), kind=kLoop, calls=%fused_computation.536 | loop fusion | flops 34015232 | bytes 9412608 | tf_op jit(solution)/shard_map/add | solution.py:54
  174.4 0.3 multiply_add_fusion.7
  174.9 0.1 fusion.403
  175.0 0.4 multiply_add_fusion
  175.3 1.0 copy.20
  (19 shorter events, 0.2 us)
Async XLA Ops:
  1.5 16.8 %copy-start = (f32[5,16,16,128]{3,2,1,0:T(8,128)S(1)}, f32[5,16,16,128]{3,2,1,0:T(8,128)}, u32[]{:S(2)}) copy-start(f32[5,16,16,128]{3,2,1,0:T(8,128)} %param.1) | copy-start | bytes 1966084
  2.1 125.7 %collective-permute-start.5 = (f32[5,16,16,3]{2,1,3,0:T(8,128)S(1)}, f32[5,16,16,3]{2,1,3,0:T(8,128)S(1)}, u32[]{:S(2)}, u32[]{:S(2)}) collective-permute-start(f32[5,16,16,3]{2,1,3,0:T(8,128)S(1)} %copy.22), channel_id=1, source_target_pairs={{1,0},{2,1},{3,2},{4,3},{5,4},{6,5},{7,6},{0,7},{9,8},{10,9},{11,1... | collective-permute-start | bytes 46088 | tf_op jit(solution)/shard_map/ppermute | solution.py:31
  16.4 115.7 %collective-permute-start.4 = (f32[5,16,16,3]{2,1,3,0:T(8,128)S(1)}, f32[5,16,16,3]{2,1,3,0:T(8,128)}, u32[]{:S(2)}, u32[]{:S(2)}) collective-permute-start(f32[5,16,16,3]{2,1,3,0:T(8,128)S(1)} %copy.21), channel_id=1, source_target_pairs={{0,1},{1,2},{2,3},{3,4},{4,5},{5,6},{6,7},{7,0},{8,9},{9,10},{10,1... | collective-permute-start | bytes 46088 | tf_op jit(solution)/shard_map/ppermute | solution.py:30
  19.2 134.5 %collective-permute-start.2 = (f32[5,16,3,128]{3,1,2,0:T(8,128)}, f32[5,16,3,128]{3,1,2,0:T(8,128)S(1)}, u32[]{:S(2)}, u32[]{:S(2)}) collective-permute-start(f32[5,16,3,128]{3,1,2,0:T(8,128)} %get-tuple-element.108), channel_id=1, source_target_pairs={{0,8},{8,16},{16,24},{24,32},{32,40},{40,48},{48,56},{56,0},{1,9},... | collective-permute-start | bytes 368648 | tf_op jit(solution)/shard_map/ppermute | solution.py:30
  21.3 132.7 %collective-permute-start.3 = (f32[5,16,3,128]{3,1,2,0:T(8,128)}, f32[5,16,3,128]{3,1,2,0:T(8,128)S(1)}, u32[]{:S(2)}, u32[]{:S(2)}) collective-permute-start(f32[5,16,3,128]{3,1,2,0:T(8,128)} %get-tuple-element.107), channel_id=1, source_target_pairs={{8,0},{16,8},{24,16},{32,24},{40,32},{48,40},{56,48},{0,56},{9,1},... | collective-permute-start | bytes 368648 | tf_op jit(solution)/shard_map/ppermute | solution.py:31
  23.6 139.0 %collective-permute-start.1 = (f32[5,3,16,128]{3,1,2,0:T(4,128)S(1)}, f32[5,3,16,128]{3,1,2,0:T(4,128)S(1)}, u32[]{:S(2)}, u32[]{:S(2)}) collective-permute-start(f32[5,3,16,128]{3,1,2,0:T(4,128)S(1)} %get-tuple-element.112), channel_id=1, source_target_pairs={{64,0},{128,64},{192,128},{256,192},{320,256},{384,320},{448,384},... | collective-permute-start | bytes 368648 | tf_op jit(solution)/shard_map/ppermute | solution.py:31
  127.8 34.8 %collective-permute-start = (f32[5,3,16,128]{3,1,2,0:T(4,128)S(1)}, f32[5,3,16,128]{3,1,2,0:T(4,128)S(1)}, u32[]{:S(2)}, u32[]{:S(2)}) collective-permute-start(f32[5,3,16,128]{3,1,2,0:T(4,128)S(1)} %get-tuple-element.111), channel_id=1, source_target_pairs={{0,64},{64,128},{128,192},{192,256},{256,320},{320,384},{384,448},... | collective-permute-start | bytes 368648 | tf_op jit(solution)/shard_map/ppermute | solution.py:30
where the time goes:
time: 179 us; the launch traced here: 176 us
  blocking collectives  85.9 us (48%)
  other arithmetic  41.9 us (23%)
  starting transfers between devices  39 us (22%)
  local copies, waits for them, and re-layouts  7.12 us (4%)
  between operations  2.41 us (1%)
    pmax x5, blocking collectives, by_axis(): shard = lax.pmax(shard, axis)  85.9 us
    add x6, other arithmetic, multiply_rows(): accum = product_term if accum is None else accum + product_term  33.7 us
    ppermute x3, starting transfers between devices, padded(): after = lax.ppermute(first, axis, down)  31.4 us
    ppermute x3, starting transfers between devices, padded(): before = lax.ppermute(last, axis, up)  7.62 us
  transfers between devices with their start and end apart: 6, of which 0 were waited for; matrix products, arithmetic and copies ran while one was open for 19% of the time, Pallas kernels for 0%

commit v1 on v0

v1 whole, which is shorter than its diff:
```python
import functools

import jax
import jax.numpy as jnp
from jax import lax
from jax.experimental import pallas as pl
from jax.experimental.pallas import tpu as pltpu
from jax.sharding import PartitionSpec as P

GAMMA = 1.4
COURANT = 0.4
EPS = 1e-06 * 4.0 * 0.75
ORDER = ((0, 1, 2, 3, 4), (0, 2, 1, 3, 4), (0, 3, 1, 2, 4))
MESH = pl.DeviceIdType.MESH
F32 = jnp.float32
ROOTS = 4
Z = 32


def rcp(x):
    return pltpu.reciprocal(x, approx=True)


def rows(start, count=16):
    return pl.ds(pl.multiple_of(start, 8), count)


def flux(q):
    inv = 1.0 / q[0]
    vn = q[1] * inv
    kin2 = (q[1] * q[1] + q[2] * q[2] + q[3] * q[3]) * inv
    p = (GAMMA - 1.0) * (q[4] - 0.5 * kin2)
    return q[1] * vn + p, q[2] * vn, q[3] * vn, (q[4] + p) * vn


def cells(qr, order, dr, lo, hi):
    def body(j, carry):
        q0 = [qr[c, rows(16 * j), :] for c in order]
        q1 = [qr[c, rows(16 * j + 16), :] for c in order]
        f0, f1 = flux(q0), flux(q1)
        for c in range(5):
            dr[c, j] = q1[c] - q0[c]
        for c in range(4):
            dr[5 + c, j] = f1[c] - f0[c]
        return carry

    lax.fori_loop(lo, hi, body, 0)


def faces(qr, order, dr, gh, co, lo, hi):
    def body(f, carry):
        m = [0.5 * (qr[c, rows(16 * f + 32), :] + qr[c, rows(16 * f + 48), :]) for c in order]
        inv = 1.0 / m[0]
        vn, va, vb = m[1] * inv, m[2] * inv, m[3] * inv
        kin = 0.5 * (vn * vn + va * va + vb * vb)
        p = (GAMMA - 1.0) * (m[4] - m[0] * kin)
        c2 = GAMMA * p * inv
        c = jnp.sqrt(c2)
        half_inv_c = 0.5 / c
        half_b1 = (0.5 * (GAMMA - 1.0)) / c2
        for i, v in enumerate((vn, va, vb, kin, c, c2 * (1.0 / (GAMMA - 1.0)))):
            co[f, i] = v
        for k in range(5):
            for w in range(2):
                if w == 0:
                    v = [dr[1, f + k]] + [dr[5 + i, f + k] for i in range(4)]
                else:
                    v = [dr[i, f + k] for i in range(5)]
                a = half_b1 * ((kin * v[0] + v[4]) - (vn * v[1] + va * v[2] + vb * v[3]))
                b = half_inv_c * (v[1] - vn * v[0])
                for i, x in enumerate(
                    (a - b, v[2] - va * v[0], v[3] - vb * v[0], v[0] - (a + a), a + b)
                ):
                    gh[f, 10 * i + 5 * w + k] = x
        return carry

    lax.fori_loop(lo, hi, body, 0)


def base(dr, rb, lo, hi):
    def body(i, carry):
        for c in range(5):
            r = 1 if c == 0 else 4 + c
            d = [dr[r, i + 1 + k] for k in range(4)]
            rb[c, i] = 7.0 * (d[1] + d[2]) - (d[0] + d[3])
            d = [dr[c, i + 1 + k] for k in range(4)]
            rb[5 + c, i] = 3.0 * (d[1] - d[2]) + (d[3] - d[0])
        return carry

    lax.fori_loop(lo, hi, body, 0)


def corr(d1, d2, d3, d4):
    s1, s2, s3 = d2 - d1, d3 - d2, d4 - d3
    a, b = 0.75 * d2, 0.75 * d3
    r0 = rcp(a * (d2 + s1) + (s1 * s1 + EPS))
    r1 = rcp(a * d3 + (s2 * s2 + EPS))
    r2 = rcp(b * (d3 - s3) + (s3 * s3 + EPS))
    w0, w1, w2 = r0 * r0, 6.0 * (r1 * r1), 3.0 * (r2 * r2)
    num = (w0 + w0) * (s1 - s2) + w2 * (s2 - s3)
    return num * rcp(w0 + w1 + w2)


def weno(gh, co, sv, d, fl, lo, hi):
    def body(f, carry):
        s = sv[d]
        kap = []
        for m in range(5):
            g = [gh[f, 10 * m + k] for k in range(5)]
            h = [s * gh[f, 10 * m + 5 + k] for k in range(5)]
            up = corr(g[0] + h[0], g[1] + h[1], g[2] + h[2], g[3] + h[3])
            down = corr(g[4] - h[4], g[3] - h[3], g[2] - h[2], g[1] - h[1])
            kap.append(up - down)
        vn, va, vb, kin, c, e = [co[f, i] for i in range(6)]
        pair = kap[0] + kap[4]
        f0 = pair + kap[3]
        cd = c * (kap[4] - kap[0])
        fl[f, 0] = f0
        fl[f, 1] = vn * f0 + cd
        fl[f, 2] = va * f0 + kap[1]
        fl[f, 3] = vb * f0 + kap[2]
        fl[f, 4] = kin * f0 + e * pair + vn * cd + va * kap[1] + vb * kap[2]
        return carry

    lax.fori_loop(lo, hi, body, 0)


def divergence(rb, fl, sv, d, c, i):
    return sv[3 + d] * (rb[c, i] + sv[d] * rb[5 + c, i] + (fl[i + 1, c] - fl[i, c]))


def kernel(
    counts, q_hbm, out_ref,
    qx, qy, qz, tz, drx, dry, drz, ghx, ghy, ghz, cox, coy, coz, rbx, rby, rbz, flx, fly, flz,
    ay, az, oz, sv, gbuf, ybuf, zbuf, fin, xs, xh, rl, yh, zh_buf,
    in_sem, sg, rg, sy, ry, sz, rz, sb, rbc, s1, r1, s2, r2, s3, r3, sh, rh,
):
    gx, gy, gz = lax.axis_index("gx"), lax.axis_index("gy"), lax.axis_index("gz")
    y, zhi = lax.rem(gx, 4), gx // 4
    z = zhi * 8 + gz

    def in_plane(yy):
        return (zhi * 4 + yy, gy, gz)

    def across(yy, step):
        return (lax.rem(zhi + 4 + step, 4) * 4 + yy, gy, gz)

    def along_z(t):
        return ((t // 8) * 4 + y, gy, lax.rem(t, 8))

    def along_gy(k):
        return (gx, lax.rem(gy + 8 + k, 8), gz)

    def along_gz(k):
        return (gx, gy, lax.rem(gz + 8 + k, 8))

    def remote(src, dst, send, recv, device):
        return pltpu.make_async_remote_copy(
            src_ref=src, dst_ref=dst, send_sem=send, recv_sem=recv, device_id=device, device_id_type=MESH
        )

    load = pltpu.make_async_copy(q_hbm, qx.at[:, pl.ds(48, 256), :], in_sem)
    load.start()

    bar = pltpu.get_barrier_semaphore()

    def tell(device):
        pl.semaphore_signal(bar, inc=1, device_id=device, device_id_type=MESH)

    for k in range(1, 8):
        tell(along_gy(k))
    for k in range(1, 4):
        tell(in_plane(lax.rem(y + k, 4)))
    tell(along_gz(1))
    tell(along_gz(-1))

    @pl.when(y == 0)
    def _():
        for c in range(4):
            tell(across(c, -1))

    @pl.when(y == 3)
    def _():
        for c in range(4):
            tell(across(c, 1))

    @pl.when(z < ROOTS)
    def _():
        def one(k, carry):
            tell(along_z(lax.rem(z + k, Z)))
            return carry

        lax.fori_loop(1, Z, one, 0)

    @pl.when(z >= ROOTS)
    def _():
        tell(along_z(1 + lax.rem(z - ROOTS + 3 * ROOTS, ROOTS - 1)))

    load.wait()

    def speeds(i, carry):
        q = [qx[c, rows(16 * i + 48), :] for c in range(5)]
        inv = 1.0 / q[0]
        v = [q[1] * inv, q[2] * inv, q[3] * inv]
        p = (GAMMA - 1.0) * (q[4] - 0.5 * q[0] * (v[0] * v[0] + v[1] * v[1] + v[2] * v[2]))
        snd = jnp.sqrt(GAMMA * p * inv)
        return tuple(jnp.maximum(m, jnp.abs(u) + snd) for m, u in zip(carry, v))

    zero = jnp.zeros((16, 128), F32)
    lane = lax.broadcasted_iota(jnp.int32, (1, 128), 1)
    local = [jnp.max(jnp.max(m, axis=0, keepdims=True), axis=1, keepdims=True) for m in lax.fori_loop(0, 16, speeds, (zero,) * 3)]
    mine = jnp.where(lane == 0, local[0], jnp.where(lane == 1, local[1], jnp.where(lane == 2, local[2], 0.0)))
    gbuf[0] = mine
    for side, first in ((0, 256), (1, 48)):
        for c in range(4):
            xs[side, c, pl.ds(0, 48), :] = qx[c, pl.ds(first, 48), :]
            xs[side, c, pl.ds(48, 16), :] = qx[4, pl.ds(first + 16 * min(c, 2), 16), :]

    targets = jnp.where(z == 0, 0, jnp.where(z == 1, 10, 9))
    pl.semaphore_wait(bar, 14 + jnp.where(z < ROOTS, ROOTS - 1 + targets, ROOTS))

    def gy_copy(k):
        return remote(gbuf.at[0], gbuf.at[k], sg.at[k], rg.at[k], along_gy(k))

    for k in range(1, 8):
        gy_copy(k).start()

    @pl.when(y == 3)
    def _():
        for c in range(3):
            remote(xs.at[0, c], rl.at[0], s2.at[c], r2.at[0], in_plane(c)).start()

    @pl.when(y == 0)
    def _():
        for c in range(1, 4):
            remote(xs.at[1, c], rl.at[1], s2.at[c], r2.at[1], in_plane(c)).start()

    for k in range(1, 8):
        gy_copy(k).wait_recv()
    ybuf[0] = jnp.max(gbuf[...].reshape(8, 128), axis=0, keepdims=True)

    def y_copy(k):
        return remote(ybuf.at[0], ybuf.at[k], sy.at[k], ry.at[k], in_plane(lax.rem(y + k, 4)))

    for k in range(1, 4):
        y_copy(k).start()
    for k in range(1, 4):
        y_copy(k).wait_recv()
    zbuf[0] = jnp.max(ybuf[...].reshape(4, 128), axis=0, keepdims=True)

    def z_copy(r):
        k = lax.rem(z - r + Z, Z)
        return remote(zbuf.at[0], zbuf.at[k], sz.at[r], rz.at[k], along_z(r))

    for r in range(ROOTS):

        @pl.when(z != r)
        def _(r=r):
            z_copy(r).start()

    def up(src):
        return remote(src, xh.at[0, y], s3.at[0], r3.at[0, y], across(0, 1))

    def down(src):
        return remote(src, xh.at[1, y], s3.at[1], r3.at[1, y], across(3, -1))

    def first_leg(i):
        return remote(xs.at[i, 0], rl.at[i], s2.at[0], r2.at[i], in_plane(y))

    @pl.when(y < 3)
    def _():
        first_leg(0).wait_recv()
        up(rl.at[0]).start()

    @pl.when(y == 3)
    def _():
        up(xs.at[0, 3]).start()

    @pl.when(y > 0)
    def _():
        first_leg(1).wait_recv()
        down(rl.at[1]).start()

    @pl.when(y == 0)
    def _():
        down(xs.at[1, 0]).start()

    def near(i):
        return remote(xs.at[i], xh.at[i], s1.at[i], r1.at[i], in_plane(lax.rem(y + 4 + (1 - 2 * i), 4)))

    @pl.when(y < 3)
    def _():
        near(0).start()

    @pl.when(y > 0)
    def _():
        near(1).start()

    for c in range(5):

        def turn(j, carry, c=c):
            qy[c, rows(16 * j + 48), :] = qx[c, pl.ds(48 + j, 16, stride=16), :]
            return carry

        lax.fori_loop(0, 16, turn, 0)

    def y_halo(i):
        src = qy.at[:, pl.ds(256 if i == 0 else 48, 48), :]
        return remote(src, yh.at[i], sh.at[i], rh.at[i], along_gy(1 - 2 * i))

    y_halo(0).start()
    y_halo(1).start()

    def flip(k, carry):
        block = qx[k // 2, rows(48 + 128 * lax.rem(k, 2), 128), :]
        tz[k, pl.ds(8, 128), :] = block.T
        return carry

    lax.fori_loop(0, 10, flip, 0)

    def z_halo(i):
        src = tz.at[:, pl.ds(128 if i == 0 else 8, 8), :]
        return remote(src, zh_buf.at[i], sh.at[2 + i], rh.at[2 + i], along_gz(1 - 2 * i))

    z_halo(0).start()
    z_halo(1).start()

    cells(qx, ORDER[0], drx, 3, 18)
    faces(qx, ORDER[0], drx, ghx, cox, 3, 14)
    base(drx, rbx, 2, 14)

    y_halo(0).wait_recv()
    y_halo(1).wait_recv()
    qy[:, pl.ds(0, 48), :] = yh[0]
    qy[:, pl.ds(304, 48), :] = yh[1]
    cells(qy, ORDER[1], dry, 0, 21)
    faces(qy, ORDER[1], dry, ghy, coy, 0, 17)
    base(dry, rby, 0, 16)

    z_halo(0).wait_recv()
    z_halo(1).wait_recv()
    z_halo(0).wait_send()
    z_halo(1).wait_send()
    tz[:, pl.ds(5, 3), :] = zh_buf[0, :, pl.ds(5, 3), :]
    tz[:, pl.ds(136, 3), :] = zh_buf[1, :, pl.ds(0, 3), :]
    for c in range(5):

        def line(j, carry, c=c):
            qz[c, rows(16 * j, 8), :] = tz[2 * c, pl.ds(5 + j, 8, stride=16), :]
            qz[c, rows(16 * j + 8, 8), :] = tz[2 * c + 1, pl.ds(5 + j, 8, stride=16), :]
            return carry

        lax.fori_loop(0, 22, line, 0)
    cells(qz, ORDER[2], drz, 0, 21)
    faces(qz, ORDER[2], drz, ghz, coz, 0, 17)
    base(drz, rbz, 0, 16)

    def spread(i):
        t = ROOTS + (ROOTS - 1) * i + z - 1
        return t, remote(fin.at[0], fin.at[1], sb.at[i], rbc.at[0], along_z(lax.rem(t + Z, Z)))

    @pl.when(z < ROOTS)
    def _():
        def arrived(k, carry):
            remote(zbuf.at[0], zbuf.at[k], sz.at[0], rz.at[k], along_z(z)).wait_recv()
            return carry

        lax.fori_loop(1, Z, arrived, 0)
        top = jnp.max(zbuf[...].reshape(Z, 128), axis=0, keepdims=True)
        fin[0] = top
        fin[1] = top

        @pl.when(z > 0)
        def _():
            for i in range(10):
                t, copy = spread(i)

                @pl.when(t < Z)
                def _(copy=copy):
                    copy.start()

    @pl.when(z >= ROOTS)
    def _():
        spread(0)[1].wait_recv()

    row = fin[1]
    s = [jnp.max(jnp.where(lane == d, row, 0.0), axis=1, keepdims=True) for d in range(3)]
    step = COURANT / (s[0] * counts[0] + s[1] * counts[1] + s[2] * counts[2])
    for d in range(3):
        sv[d] = jnp.broadcast_to(s[d], (16, 128))
        sv[3 + d] = jnp.broadcast_to(step * (counts[d] / 12.0), (16, 128))

    weno(ghz, coz, sv, 2, flz, 0, 17)

    def close_z(i, carry):
        for c in range(5):
            az[ORDER[2][c], rows(16 * i), :] = divergence(rbz, flz, sv, 2, c, i)
        return carry

    lax.fori_loop(0, 16, close_z, 0)

    def unflip(k, carry):
        c, half = k // 2, lax.rem(k, 2)
        parts = [az[c, pl.ds(half * 8 + i, 16, stride=16), :] for i in range(8)]
        oz[c, rows(128 * half, 128), :] = jnp.concatenate(parts, axis=0).T
        return carry

    lax.fori_loop(0, 10, unflip, 0)
    weno(ghy, coy, sv, 1, fly, 0, 17)

    def close_y(i, carry):
        for c in range(5):
            ay[ORDER[1][c], rows(16 * i), :] = divergence(rby, fly, sv, 1, c, i)
        return carry

    lax.fori_loop(0, 16, close_y, 0)
    weno(ghx, cox, sv, 0, flx, 3, 14)

    @pl.when(y > 0)
    def _():
        near(0).wait_recv()

    @pl.when(y == 0)
    def _():
        for c in range(4):
            remote(rl.at[0], xh.at[0, c], s3.at[0], r3.at[0, c], across(0, 1)).wait_recv()

    @pl.when(y < 3)
    def _():
        near(1).wait_recv()

    @pl.when(y == 3)
    def _():
        for c in range(4):
            remote(rl.at[0], xh.at[1, c], s3.at[1], r3.at[1, c], across(0, 1)).wait_recv()

    for side, first in ((0, 0), (1, 304)):
        for c in range(4):
            qx[c, pl.ds(first, 48), :] = xh[side, c, pl.ds(0, 48), :]
        for i in range(3):
            qx[4, pl.ds(first + 16 * i, 16), :] = xh[side, i, pl.ds(48, 16), :]
    for lo, hi, flo, fhi in ((0, 3, 0, 3), (18, 21, 14, 17)):
        cells(qx, ORDER[0], drx, lo, hi)
        faces(qx, ORDER[0], drx, ghx, cox, flo, fhi)
        weno(ghx, cox, sv, 0, flx, flo, fhi)
    base(drx, rbx, 0, 2)
    base(drx, rbx, 14, 16)

    def close(i, carry):
        for c in range(5):
            total = divergence(rbx, flx, sv, 0, c, i) + ay[c, pl.ds(i, 16, stride=16), :] + oz[c, rows(16 * i), :]
            out_ref[c, rows(16 * i), :] = qx[c, rows(16 * i + 48), :] - total
        return carry

    lax.fori_loop(0, 16, close, 0)

    for k in range(1, 8):
        gy_copy(k).wait_send()
    for k in range(1, 4):
        y_copy(k).wait_send()
    for r in range(ROOTS):

        @pl.when(z != r)
        def _(r=r):
            z_copy(r).wait_send()

    @pl.when(y == 3)
    def _():
        for c in range(3):
            remote(xs.at[0, c], rl.at[0], s2.at[c], r2.at[0], in_plane(c)).wait_send()

    @pl.when(y == 0)
    def _():
        for c in range(1, 4):
            remote(xs.at[1, c], rl.at[1], s2.at[c], r2.at[1], in_plane(c)).wait_send()

    up(rl.at[0]).wait_send()
    down(rl.at[1]).wait_send()

    @pl.when(y < 3)
    def _():
        near(0).wait_send()

    @pl.when(y > 0)
    def _():
        near(1).wait_send()

    y_halo(0).wait_send()
    y_halo(1).wait_send()

    @pl.when(jnp.logical_and(z > 0, z < ROOTS))
    def _():
        for i in range(10):
            t, copy = spread(i)

            @pl.when(t < Z)
            def _(copy=copy):
                copy.wait_send()


def per_device(conserved):
    counts = [
        float(n * lax.axis_size(a)) for n, a in zip(conserved.shape[1:], ("gx", "gy", "gz"))
    ]
    vm = lambda *shape: pltpu.VMEM(shape, F32)
    dma = lambda *shape: pltpu.SemaphoreType.DMA(shape)
    scratch = (
        [vm(5, 352, 128)] * 3 + [vm(10, 144, 128)] + [vm(9, 21, 16, 128)] * 3
        + [vm(17, 50, 16, 128)] * 3 + [vm(17, 6, 16, 128)] * 3 + [vm(10, 16, 16, 128)] * 3
        + [vm(17, 5, 16, 128)] * 3 + [vm(5, 256, 128)] * 3 + [vm(6, 16, 128)]
        + [vm(8, 1, 128), vm(4, 1, 128), vm(Z, 1, 128), vm(2, 1, 128)]
        + [vm(2, 4, 64, 128), vm(2, 4, 64, 128), vm(2, 64, 128), vm(2, 5, 48, 128), vm(2, 10, 8, 128)]
        + [pltpu.SemaphoreType.DMA, dma(8), dma(8), dma(4), dma(4), dma(ROOTS), dma(Z), dma(10), dma(1)]
        + [dma(2), dma(2), dma(4), dma(2), dma(2), dma(2, 4), dma(4), dma(4)]
    )
    flat = conserved.reshape(5, 256, 128)
    out = pl.pallas_call(
        functools.partial(kernel, counts),
        out_shape=jax.ShapeDtypeStruct(flat.shape, F32),
        in_specs=[pl.BlockSpec(memory_space=pl.ANY)],
        out_specs=pl.BlockSpec(memory_space=pltpu.VMEM),
        scratch_shapes=scratch,
        compiler_params=pltpu.CompilerParams(
            collective_id=0, has_side_effects=True, vmem_limit_bytes=60 * 2**20
        ),
        name="weno_section",
    )(flat)
    return out.reshape(conserved.shape)


def solution(mesh):
    spec = P(None, "gx", "gy", "gz")
    return jax.shard_map(
        per_device, mesh=mesh, in_specs=(spec,), out_specs=spec, check_vma=False
    )
```

time: 179 us -> 59.9 us (0.33); the launches traced: 176 us -> 59.6 us
  blocking collectives: 85.9 us -> 0 us
  Pallas kernels: 0 us -> 57.6 us
  other arithmetic: 41.9 us -> 0 us
  starting transfers between devices: 39 us -> 0 us
  local copies, waits for them, and re-layouts: 7.12 us -> 1.99 us
  between operations: 2.41 us -> 0.01 us
    pmax x5 -> x0, blocking collectives: 85.9 us -> none  [by_axis(): shard = lax.pmax(shard, axis)]
    pallas_call x0 -> x1, Pallas kernels: none -> 57.6 us  [per_device(): pl.pallas_call(functools.partial(kernel, counts), out_shape=jax.ShapeDtyp...]
    ppermute x6 -> x0, starting transfers between devices: 39 us -> none  [the longest x3 31.4 us: padded(): after = lax.ppermute(first, axis, down)]
    add x7 -> x0, other arithmetic: 34.1 us -> none  [the longest x6 33.7 us: multiply_rows(): accum = product_term if accum is None else accum + product_term]
    mul x6 -> x0, other arithmetic: 5.24 us -> none  [the longest x3 2.82 us: face_divergence(): 0.5 * (flux + wave_speed * component)]
    slice x3 -> x0, local copies, waits for them, and re-layouts: 2.27 us -> none  [the longest x2 1.58 us: padded(): last = lax.slice_in_dim(shard, length - width, length, axis=dim)]
    ppermute x2 -> x0, local copies, waits for them, and re-layouts: 2 us -> none  [the longest x1 1.44 us: padded(): before = lax.ppermute(last, axis, up)]
  transfers between devices with their start and end apart: 6 -> 0, of which waited for: 0 -> 0; matrix products, arithmetic and copies ran while one was open for 19% -> 0% of each run, Pallas kernels for 0% -> 0%
where the time goes in v1:
time: 59.9 us; the launch traced here: 59.6 us
  Pallas kernels  57.6 us (96%)
  local copies, waits for them, and re-layouts  1.99 us (3%)
    pallas_call x1, Pallas kernels, per_device(): pl.pallas_call(functools.partial(kernel, counts), out_shape=jax.ShapeDtyp...  57.6 us
    unnamed x1, local copies, waits for them, and re-layouts  1.99 us

profile of v1, /device:TPU:1, one launch (start us, length us, event | category | flops | bytes accessed | tf_op | source)
XLA Modules:
  0.0 59.6 jit_solution(10716265071278502618)
XLA Ops:
  0.0 57.6 %weno_section.1 = f32[5,256,128]{2,1,0:T(8,128)} custom-call(f32[5,256,128]{2,1,0:T(8,128)} %bitcast.3), custom_call_target="tpu_custom_call" | custom-call | tf_op jit(solution)/shard_map/weno_section/pallas_call | solution.py:517
  57.6 2.0 %copy.3 = f32[5,16,16,128]{3,2,1,0:T(8,128)} copy(f32[5,16,16,128]{3,2,1,0:T(8,128)} %bitcast.2) | data formatting | bytes 1310720

commit v2 on v1

--- a/solution.py
+++ b/solution.py
@@ -101,8 +101,10 @@
     return num * rcp(w0 + w1 + w2)
 
 
-def weno(gh, co, sv, d, fl, lo, hi):
+def weno(gh, co, sv, d, fl, lo, hi, also=None):
     def body(f, carry):
+        if also is not None:
+            also(f)
         s = sv[d]
         kap = []
         for m in range(5):
@@ -132,8 +134,8 @@
 def kernel(
     counts, q_hbm, out_ref,
     qx, qy, qz, tz, drx, dry, drz, ghx, ghy, ghz, cox, coy, coz, rbx, rby, rbz, flx, fly, flz,
-    ay, az, oz, sv, gbuf, ybuf, zbuf, fin, xs, xh, rl, yh, zh_buf,
-    in_sem, sg, rg, sy, ry, sz, rz, sb, rbc, s1, r1, s2, r2, s3, r3, sh, rh,
+    ay, az, oz, sv, gbuf, zbuf, fin, xs, xh, rl, yh, zh_buf,
+    in_sem, sg, rg, sz, rz, sb, rbc, s1, r1, s2, r2, s3, r3, sh, rh,
 ):
     gx, gy, gz = lax.axis_index("gx"), lax.axis_index("gy"), lax.axis_index("gz")
     y, zhi = lax.rem(gx, 4), gx // 4
@@ -147,6 +149,9 @@
 
     def along_z(t):
         return ((t // 8) * 4 + y, gy, lax.rem(t, 8))
+
+    def at(yy, t):
+        return ((t // 8) * 4 + yy, gy, lax.rem(t, 8))
 
     def along_gy(k):
         return (gx, lax.rem(gy + 8 + k, 8), gz)
@@ -187,10 +192,10 @@
     @pl.when(z < ROOTS)
     def _():
         def one(k, carry):
-            tell(along_z(lax.rem(z + k, Z)))
+            tell(at(lax.rem(y + k, 4), lax.rem(z + k // 4, Z)))
             return carry
 
-        lax.fori_loop(1, Z, one, 0)
+        lax.fori_loop(4, 4 * Z, one, 0)
 
     @pl.when(z >= ROOTS)
     def _():
@@ -217,7 +222,7 @@
             xs[side, c, pl.ds(48, 16), :] = qx[4, pl.ds(first + 16 * min(c, 2), 16), :]
 
     targets = jnp.where(z == 0, 0, jnp.where(z == 1, 10, 9))
-    pl.semaphore_wait(bar, 14 + jnp.where(z < ROOTS, ROOTS - 1 + targets, ROOTS))
+    pl.semaphore_wait(bar, 14 + jnp.where(z < ROOTS, 4 * (ROOTS - 1) + targets, 4 * ROOTS))
 
     def gy_copy(k):
         return remote(gbuf.at[0], gbuf.at[k], sg.at[k], rg.at[k], along_gy(k))
@@ -237,26 +242,19 @@
 
     for k in range(1, 8):
         gy_copy(k).wait_recv()
-    ybuf[0] = jnp.max(gbuf[...].reshape(8, 128), axis=0, keepdims=True)
-
-    def y_copy(k):
-        return remote(ybuf.at[0], ybuf.at[k], sy.at[k], ry.at[k], in_plane(lax.rem(y + k, 4)))
-
-    for k in range(1, 4):
-        y_copy(k).start()
-    for k in range(1, 4):
-        y_copy(k).wait_recv()
-    zbuf[0] = jnp.max(ybuf[...].reshape(4, 128), axis=0, keepdims=True)
-
-    def z_copy(r):
-        k = lax.rem(z - r + Z, Z)
-        return remote(zbuf.at[0], zbuf.at[k], sz.at[r], rz.at[k], along_z(r))
+    zbuf[0] = jnp.max(gbuf[...], axis=0)
+
+    def z_copy(r, k):
+        slot = 4 * lax.rem(z - r + Z, Z) + (4 - k) % 4
+        return remote(zbuf.at[0], zbuf.at[slot], sz.at[4 * r + k], rz.at[0], at(lax.rem(y + k, 4), r))
 
     for r in range(ROOTS):
+        for k in range(1, 4):
+            z_copy(r, k).start()
 
         @pl.when(z != r)
         def _(r=r):
-            z_copy(r).start()
+            z_copy(r, 0).start()
 
     def up(src):
         return remote(src, xh.at[0, y], s3.at[0], r3.at[0, y], across(0, 1))
@@ -266,24 +264,6 @@
 
     def first_leg(i):
         return remote(xs.at[i, 0], rl.at[i], s2.at[0], r2.at[i], in_plane(y))
-
-    @pl.when(y < 3)
-    def _():
-        first_leg(0).wait_recv()
-        up(rl.at[0]).start()
-
-    @pl.when(y == 3)
-    def _():
-        up(xs.at[0, 3]).start()
-
-    @pl.when(y > 0)
-    def _():
-        first_leg(1).wait_recv()
-        down(rl.at[1]).start()
-
-    @pl.when(y == 0)
-    def _():
-        down(xs.at[1, 0]).start()
 
     def near(i):
         return remote(xs.at[i], xh.at[i], s1.at[i], r1.at[i], in_plane(lax.rem(y + 4 + (1 - 2 * i), 4)))
@@ -324,6 +304,24 @@
 
     z_halo(0).start()
     z_halo(1).start()
+
+    @pl.when(y < 3)
+    def _():
+        first_leg(0).wait_recv()
+        up(rl.at[0]).start()
+
+    @pl.when(y == 3)
+    def _():
+        up(xs.at[0, 3]).start()
+
+    @pl.when(y > 0)
+    def _():
+        first_leg(1).wait_recv()
+        down(rl.at[1]).start()
+
+    @pl.when(y == 0)
+    def _():
+        down(xs.at[1, 0]).start()
 
     cells(qx, ORDER[0], drx, 3, 18)
     faces(qx, ORDER[0], drx, ghx, cox, 3, 14)
@@ -361,12 +359,9 @@
 
     @pl.when(z < ROOTS)
     def _():
-        def arrived(k, carry):
-            remote(zbuf.at[0], zbuf.at[k], sz.at[0], rz.at[k], along_z(z)).wait_recv()
-            return carry
-
-        lax.fori_loop(1, Z, arrived, 0)
-        top = jnp.max(zbuf[...].reshape(Z, 128), axis=0, keepdims=True)
+        others = zbuf.at[pl.ds(1, 4 * Z - 1)]
+        remote(others, others, sz.at[0], rz.at[0], along_z(z)).wait_recv()
+        top = jnp.max(zbuf[...], axis=0)
         fin[0] = top
         fin[1] = top
 
@@ -399,14 +394,13 @@
 
     lax.fori_loop(0, 16, close_z, 0)
 
-    def unflip(k, carry):
+    def unflip(k):
         c, half = k // 2, lax.rem(k, 2)
         parts = [az[c, pl.ds(half * 8 + i, 16, stride=16), :] for i in range(8)]
         oz[c, rows(128 * half, 128), :] = jnp.concatenate(parts, axis=0).T
-        return carry
-
-    lax.fori_loop(0, 10, unflip, 0)
-    weno(ghy, coy, sv, 1, fly, 0, 17)
+
+    weno(ghy, coy, sv, 1, fly, 0, 10, unflip)
+    weno(ghy, coy, sv, 1, fly, 10, 17)
 
     def close_y(i, carry):
         for c in range(5):
@@ -456,13 +450,13 @@
 
     for k in range(1, 8):
         gy_copy(k).wait_send()
-    for k in range(1, 4):
-        y_copy(k).wait_send()
     for r in range(ROOTS):
+        for k in range(1, 4):
+            z_copy(r, k).wait_send()
 
         @pl.when(z != r)
         def _(r=r):
-            z_copy(r).wait_send()
+            z_copy(r, 0).wait_send()
 
     @pl.when(y == 3)
     def _():
@@ -508,9 +502,9 @@
         [vm(5, 352, 128)] * 3 + [vm(10, 144, 128)] + [vm(9, 21, 16, 128)] * 3
         + [vm(17, 50, 16, 128)] * 3 + [vm(17, 6, 16, 128)] * 3 + [vm(10, 16, 16, 128)] * 3
         + [vm(17, 5, 16, 128)] * 3 + [vm(5, 256, 128)] * 3 + [vm(6, 16, 128)]
-        + [vm(8, 1, 128), vm(4, 1, 128), vm(Z, 1, 128), vm(2, 1, 128)]
+        + [vm(8, 1, 128), vm(4 * Z, 1, 128), vm(2, 1, 128)]
         + [vm(2, 4, 64, 128), vm(2, 4, 64, 128), vm(2, 64, 128), vm(2, 5, 48, 128), vm(2, 10, 8, 128)]
-        + [pltpu.SemaphoreType.DMA, dma(8), dma(8), dma(4), dma(4), dma(ROOTS), dma(Z), dma(10), dma(1)]
+        + [pltpu.SemaphoreType.DMA, dma(8), dma(8), dma(4 * ROOTS), dma(1), dma(10), dma(1)]
         + [dma(2), dma(2), dma(4), dma(2), dma(2), dma(2, 4), dma(4), dma(4)]
     )
     flat = conserved.reshape(5, 256, 128)
@@ -521,10 +515,10 @@
         out_specs=pl.BlockSpec(memory_space=pltpu.VMEM),
         scratch_shapes=scratch,
         compiler_params=pltpu.CompilerParams(
-            collective_id=0, has_side_effects=True, vmem_limit_bytes=60 * 2**20
+            collective_id=0, has_side_effects=True, vmem_limit_bytes=48 * 2**20
         ),
         name="weno_section",
-    )(flat)
+    )(pltpu.with_memory_space_constraint(flat, pltpu.HBM))
     return out.reshape(conserved.shape)
 
 

time: 59.9 us -> 54.4 us (0.908)
  Pallas kernels: 57.6 us -> 53.4 us
  local copies, waits for them, and re-layouts: 1.99 us -> 0.84 us
    pallas_call x1, Pallas kernels: 57.6 us -> 53.4 us  [per_device(): pl.pallas_call(functools.partial(kernel, counts), out_shape=jax.ShapeDtyp...]
    unnamed x1, local copies, waits for them, and re-layouts: 1.99 us -> 0.84 us
where the time goes in v2:
time: 54.4 us; the launch traced here: 54.2 us
  Pallas kernels  53.4 us (98%)
  local copies, waits for them, and re-layouts  0.84 us (2%)
    pallas_call x1, Pallas kernels, per_device(): pl.pallas_call(functools.partial(kernel, counts), out_shape=jax.ShapeDtyp...  53.4 us

profile of v2, /device:TPU:1, one launch (start us, length us, event | category | flops | bytes accessed | tf_op | source)
XLA Modules:
  0.0 54.2 jit_solution(9571825012844164588)
XLA Ops:
  0.0 53.4 %weno_section.1 = f32[5,256,128]{2,1,0:T(8,128)S(1)} custom-call(f32[5,256,128]{2,1,0:T(8,128)} %bitcast.3), custom_call_target="tpu_custom_call" | custom-call | tf_op jit(solution)/shard_map/weno_section/pallas_call | solution.py:511
  53.4 0.8 %copy.3 = f32[5,16,16,128]{3,2,1,0:T(8,128)} copy(f32[5,16,16,128]{3,2,1,0:T(8,128)S(1)} %bitcast.2) | data formatting | bytes 1310720
